TPU v7x, 32 devices: a whole 2x2x4 slice. The times are simulated.
32 devices in a mesh: section: 2 (over y), dp: 16 (over z, x, core).
Axes of the slice: x: 2, y: 2, z: 4, core: 2. Of those that a mesh axis runs over, the one named last changes fastest.
Arguments:
- activations: bfloat16 [2, 8, 256, 3584], P('section', None, 'dp'), may hold values from -8 to 8
- cotangent: bfloat16 [2, 8, 256, 3584], P('section', None, 'dp'), may hold values from -96 to 96
- target_ids: int32 [8, 256], P(None, 'dp'), may hold values from -100 to 152063, as said below
- w_gate: bfloat16 [2, 3584, 96], P('section'), may hold values from -0.09375 to 0.09375
- w_up: bfloat16 [2, 3584, 96], P('section'), may hold values from -0.09375 to 0.09375
- w_down: bfloat16 [2, 96, 3584], P('section'), may hold values from -0.625 to 0.625
Outputs:
- grad_gate: float32 [2, 3584, 96], P('section', 'dp')
- grad_up: float32 [2, 3584, 96], P('section', 'dp')
- grad_down: float32 [2, 96, 3584], P('section', None, 'dp')
- grad_rms: float32 [], replicated
Inputs may be any that keep to these rules, and one draw needn't show every extreme that they name: `target_ids`: each entry is -100 (an ignored position) or a token id in 0 to 152063; the share of ignored positions differs between the blocks of 16 tokens of different replicas, from none to about eleven sixteenths.
All inputs are finite; a program needn't handle non-finite values.
Results may differ from a plain program's by a relative error of at most 0.0015.
Values sent between devices are 32-bit elements.
A program may use at most 64 MiB of HBM per device.

v0:
```python
import jax
import jax.numpy as jnp
from jax import lax
from jax.sharding import PartitionSpec as P


def own_rows(product, span, axis):
    everything = product(jnp.int32(0), lax.axis_size(axis) * span)
    own = lax.psum_scatter(everything, axis, scatter_dimension=0, tiled=True)
    return own


def finalize_totals(product):
    rounded = lax.optimization_barrier(product.astype(jnp.bfloat16))
    return jnp.sum(rounded.astype(jnp.float32), axis=0)


def combine_sums(values):
    replica_total = lax.psum(values, "dp")
    return lax.psum(replica_total, "section")


def shards(activations, cotangent, target_ids, w_gate, w_up, w_down):
    inputs_local = activations[0]
    valid = target_ids >= 0
    local_count = jnp.sum(valid.astype(jnp.float32))
    upstream = cotangent[0] * valid.astype(jnp.bfloat16)[:, :, None]
    gate_weight = w_gate[0]
    up_weight = w_up[0]
    down_weight = w_down[0]
    width = gate_weight.shape[1]
    model_width = inputs_local.shape[2]
    count = lax.psum(local_count, "dp")
    gate = jnp.einsum("mtd,dh->mth", inputs_local, gate_weight, preferred_element_type=jnp.float32)
    up = jnp.einsum("mtd,dh->mth", inputs_local, up_weight, preferred_element_type=jnp.float32)
    sigmoid_gate = jax.nn.sigmoid(gate)
    activated = gate * sigmoid_gate
    inner_activation = (activated * up).astype(jnp.bfloat16)
    hidden_grad = jnp.einsum(
        "mtd,hd->mth", upstream, down_weight, preferred_element_type=jnp.float32
    )
    gate_grad = (hidden_grad * up * sigmoid_gate * (1.0 + gate * (1.0 - sigmoid_gate))).astype(
        jnp.bfloat16
    )
    up_grad = (hidden_grad * activated).astype(jnp.bfloat16)

    def block_terms(start, count_rows):
        input_rows = lax.dynamic_slice_in_dim(inputs_local, start, count_rows, 2)
        incoming_gradient_lines = lax.dynamic_slice_in_dim(upstream, start, count_rows, 2)
        part_gate = finalize_totals(
            jnp.einsum("mtc,mth->mch", input_rows, gate_grad, preferred_element_type=jnp.float32)
        )
        part_up = finalize_totals(
            jnp.einsum("mtc,mth->mch", input_rows, up_grad, preferred_element_type=jnp.float32)
        )
        partial_lowering_weight = finalize_totals(
            jnp.einsum(
                "mth,mtc->mch",
                inner_activation,
                incoming_gradient_lines,
                preferred_element_type=jnp.float32,
            )
        )
        return jnp.concatenate([part_gate, part_up, partial_lowering_weight], axis=1)

    summed = own_rows(block_terms, model_width // lax.axis_size("dp"), "dp")
    entries = jnp.float32(lax.axis_size("section") * 3 * model_width * width)
    scaled = summed / count
    squares = jnp.sum(scaled * scaled)
    totals = combine_sums(squares[None])
    grad_rms = jnp.sqrt(totals[0] / entries)
    grad_gate = scaled[:, :width][None]
    grad_up = scaled[:, width : 2 * width][None]
    grad_down = jnp.transpose(scaled[:, 2 * width :])[None]
    return (grad_gate, grad_up, grad_down, grad_rms)


def solution(mesh):
    in_specs = (
        P("section", None, "dp", None),
        P("section", None, "dp", None),
        P(None, "dp"),
        P("section", None, None),
        P("section", None, None),
        P("section", None, None),
    )
    out_specs = (P("section", "dp", None), P("section", "dp", None), P("section", None, "dp"), P())
    return jax.shard_map(shards, mesh=mesh, in_specs=in_specs, out_specs=out_specs, check_vma=False)
```

profile of v0, /device:TPU:0, one launch (start us, length us, event | category | flops | bytes accessed | tf_op | source)
XLA Modules:
  0.0 160.3 jit_solution(7090689319286886474)
XLA Ops:
  7.2 0.0 copy-start
  7.2 0.0 reduce-scatter.4.cloned.1.call-start
  7.2 1.4 convert_reduce_fusion.3
  8.6 0.0 copy-done
  8.6 0.0 copy-start.1
  8.6 1.6 fusion.4
  10.2 1.5 fusion.6
  11.7 1.8 %fusion.8 = f32[8,16,96]{2,1,0:T(8,128)S(1)} fusion(bf16[1,8,16,3584]{3,2,1,0:T(8,128)(2,1)} %param.7, bf16[1,96,3584]{2,1,0:T(8,128)(2,1)} %param.11, bf16[8,16]{1,0:T(8,128)(2,1)S(1)} %convert_element_type.39), kind=kOutput, calls=%fused_computation.16 | convolution fusion | flops 88539136 | bytes 1655040 | tf_op jit(solution)/shard_map/mtd,hd->mth/dot_general | solution.py:39
  13.5 1.6 %fusion.1 = bf16[8,3584,96]{1,2,0:T(8,128)(2,1)S(1)} fusion(bf16[1,8,16,3584]{3,2,1,0:T(8,128)(2,1)S(1)} %copy-done, f32[8,16,96]{2,1,0:T(8,128)S(1)} %fusion.8, f32[8,16,96]{2,1,0:T(8,128)S(1)} %fusion.4), kind=kOutput, calls=%fused_computation.7 | convolution fusion | flops 90906624 | bytes 6520832 | tf_op jit(solution)/shard_map/mtc,mth->mch/dot_general | solution.py:54
  15.1 0.0 copy-done.1
  15.1 1.6 %convolution_convert_fusion = bf16[8,3584,96]{1,2,0:T(8,128)(2,1)S(1)} fusion(bf16[1,8,16,3584]{3,2,1,0:T(8,128)(2,1)S(1)} %copy-done.1, bf16[8,16]{1,0:T(8,128)(2,1)S(1)} %convert_element_type.39, f32[8,16,96]{2,1,0:T(8,128)S(1)} %fusion.6, f32[8,16,96]{2,1,0:T(8,128)S(1)} %fusion.4), kind=kOutput, calls=%fused_computation.3 | convolution fusion | flops 91365376 | bytes 6521088 | tf_op jit(solution)/shard_map/mth,mtc->mch/dot_general | solution.py:57
  16.8 1.6 %fusion = bf16[8,3584,96]{1,2,0:T(8,128)(2,1)S(1)} fusion(bf16[1,8,16,3584]{3,2,1,0:T(8,128)(2,1)S(1)} %copy-done, f32[8,16,96]{2,1,0:T(8,128)S(1)} %fusion.4, f32[8,16,96]{2,1,0:T(8,128)S(1)} %fusion.8, f32[8,16,96]{2,1,0:T(8,128)S(1)} %fusion.6), kind=kOutput, calls=%fused_computation.6 | convolution fusion | flops 90955776 | bytes 6569984 | tf_op jit(solution)/shard_map/mtc,mth->mch/dot_general | solution.py:51
  18.4 0.8 convert_reduce_fusion.2
  19.2 1.6 %convert_reduce_fusion = (f32[3584,96]{0,1:T(8,128)S(1)}, f32[3584,96]{0,1:T(8,128)S(1)}) fusion(bf16[8,3584,96]{1,2,0:T(8,128)(2,1)S(1)} %convolution_convert_fusion, bf16[8,3584,96]{1,2,0:T(8,128)(2,1)S(1)} %fusion.1), kind=kLoop, calls=%fused_computation | loop fusion | flops 10321920 | bytes 13762560 | tf_op jit(solution)/shard_map/reduce_sum | solution.py:15
  20.8 2.3 %pad_maximum_fusion = f32[3584,288]{0,1:T(8,128)} fusion(f32[3584,96]{0,1:T(8,128)S(1)} %get-tuple-element.11, f32[3584,96]{0,1:T(8,128)S(1)} %get-tuple-element.12, f32[3584,96]{0,1:T(8,128)S(1)} %convert_reduce_fusion.2), kind=kLoop, calls=%fused_computation.8 | loop fusion | flops 2064384 | bytes 8257536 | tf_op jit(solution)/shard_map/concatenate | solution.py:64
  23.1 5.8 %copy.10 = f32[3584,288]{1,0:T(8,128)} copy(f32[3584,288]{0,1:T(8,128)} %pad_maximum_fusion) | data formatting | bytes 8257536
  28.8 0.0 reduce-scatter.4.cloned.1.call-update
  28.8 35.6 %psum.21 = f32[]{:T(128)} all-reduce(f32[]{:T(128)} %get-tuple-element.6), channel_id=1, replica_groups=mesh['section'=2,'dp'=16] {'dp'}, use_global_device_ids=true, to_apply=%region_5.0 | all-reduce | flops 1 | bytes 8 | tf_op jit(solution)/shard_map/psum | solution.py:33
  64.5 47.6 %reduce-scatter.4.cloned.1.call-done = f32[224,288]{1,0:T(8,128)} async-done(((f32[3584,288]{1,0:T(8,128)}), f32[224,288]{1,0:T(8,128)}) %reduce-scatter.4.cloned.1.call-update) | async-done | bytes 258064
  112.0 1.1 copy.11
  113.1 1.3 multiply_reduce_fusion
  114.5 30.9 %psum.22 = f32[1]{0:T(128)} all-reduce(f32[1]{0:T(128)} %bitcast.15), channel_id=1, replica_groups=mesh['section'=2,'dp'=16] {'dp'}, use_global_device_ids=true, to_apply=%region_7.0 | all-reduce | flops 1 | bytes 8 | tf_op jit(solution)/shard_map/psum | solution.py:19
  145.4 0.7 slice_bitcast_fusion
  146.1 5.5 %psum.23 = f32[1]{0:T(128)} all-reduce(f32[1]{0:T(128)} %psum.22), channel_id=1, replica_groups=mesh['section'=2,'dp'=16] {'section'}, use_global_device_ids=true, to_apply=%region_8.0 | all-reduce | flops 1 | bytes 8 | tf_op jit(solution)/shard_map/psum | solution.py:20
  (1 shorter events, 0.0 us)
Async XLA Ops:
  7.2 1.4 copy-start
  7.2 104.8 %reduce-scatter.4.cloned.1.call-start = ((), (), s32[]{:S(2)}) async-start(), calls=%async_computation.1 | async-start | bytes 5849088
  8.6 6.5 %copy-start.1 = (bf16[1,8,16,3584]{3,2,1,0:T(8,128)(2,1)S(1)}, bf16[1,8,16,3584]{3,2,1,0:T(8,128)(2,1)}, u32[]{:S(2)}) copy-start(bf16[1,8,16,3584]{3,2,1,0:T(8,128)(2,1)} %param.7) | copy-start | bytes 2752516
Sparse Core Ops, SparseCore 0:
  29.0 82.9 reduce-scatter.3
where the time goes:
time: 161 us; the launch traced here: 160 us
  blocking collectives  72.1 us (45%)
  waiting for transfers between devices  47.6 us (30%)
  between operations  15.9 us (10%)
  matrix products  9.76 us (6%)
  local copies, waits for them, and re-layouts  7.61 us (5%)
  other arithmetic  7.33 us (5%)
    unnamed x2, waiting for transfers between devices  47.6 us
    psum x1, blocking collectives, shards(): count = lax.psum(local_count, 'dp')  35.6 us
    psum x1, blocking collectives, combine_sums(): replica_total = lax.psum(values, 'dp')  30.9 us
    unnamed x6, local copies, waits for them, and re-layouts  6.9 us
    psum x1, blocking collectives, combine_sums(): return lax.psum(replica_total, 'section')  5.54 us
  transfers between devices with their start and end apart: 1, of which 1 were waited for; matrix products, arithmetic and copies ran while one was open for 0% of the time, Pallas kernels for 0%

commit v1 on v0

--- a/solution.py
+++ b/solution.py
@@ -1,7 +1,355 @@
+import functools
+
 import jax
 import jax.numpy as jnp
 from jax import lax
+from jax.experimental import pallas as pl
+from jax.experimental.pallas import tpu as pltpu
 from jax.sharding import PartitionSpec as P
+
+MESH = pl.DeviceIdType.MESH
+LANES = 128
+PIECES = 3
+
+
+def line_order(line):
+    return [sorted(range(line), key=lambda to: (-abs(to - at), -abs(2 * to - line + 1), to)) for at in range(line)]
+
+
+def looked_up(table, at, step):
+    picked = jnp.int32(0)
+    for row, entries in enumerate(table):
+        for column, entry in enumerate(entries):
+            picked = jnp.where((at == row) & (step == column), jnp.int32(entry), picked)
+    return picked
+
+
+def lane_window(tiles, offset, count):
+    first, shift = offset // LANES, offset % LANES
+    if shift == 0:
+        return tiles[first : first + count]
+    lane = lax.broadcasted_iota(jnp.int32, tiles[0].shape, 1)
+    turned = [pltpu.roll(tile, LANES - shift, 1) for tile in tiles[first : first + count + 1]]
+    turned = turned + [turned[-1]]
+    return [jnp.where(lane < LANES - shift, turned[i], turned[i + 1]) for i in range(count)]
+
+
+def kernel(
+    line, entries,
+    ids_ref, acts_ref, cot_ref, wg_ref, wu_ref, wd_ref,
+    out_ref, rms_ref,
+    masked, stage, pair_in, x_out, x_in, total, z_in, full, counts, squares, row_count, row_square,
+    pair_send, pair_recv, x_send, x_recv, z_send, z_recv, full_send, full_recv,
+    count_send, count_recv, square_send, square_recv,
+):
+    section, me = lax.axis_index("section"), lax.axis_index("dp")
+    sections, replicas = lax.axis_size("section"), lax.axis_size("dp")
+    everyone = sections * replicas
+    mine = section * replicas + me
+    core, x, z = me % 2, (me // 2) % 2, me // 4
+    micro, tokens = ids_ref.shape
+    columns = micro * tokens
+    width = wg_ref.shape[1]
+    rows = 3 * width
+    half = stage.shape[1] // 2
+    piece = half // PIECES
+    tiles = acts_ref.shape[1] // line // LANES
+    whole = tiles // 2
+    order = line_order(line)
+    pair = (section, me + 1 - 2 * core)
+    across = (section, me + 2 - 4 * x)
+
+    barrier = pltpu.get_barrier_semaphore()
+
+    def greet(step, carry):
+        other = (mine + step) % everyone
+        pl.semaphore_signal(barrier, inc=1, device_id=(other // replicas, other % replicas), device_id_type=MESH)
+        return carry
+
+    lax.fori_loop(1, everyone, greet, 0)
+
+    valid = (ids_ref[...] >= 0).astype(jnp.float32)
+    spread = (
+        lax.broadcasted_iota(jnp.int32, (tokens, columns), 1) % tokens
+        == lax.broadcasted_iota(jnp.int32, (tokens, columns), 0)
+    ).astype(jnp.float32)
+    own_micro = (
+        lax.broadcasted_iota(jnp.int32, (micro, columns), 1) // tokens
+        == lax.broadcasted_iota(jnp.int32, (micro, columns), 0)
+    )
+    laid = jnp.dot(valid, spread, preferred_element_type=jnp.float32)
+    mask = jnp.where(own_micro, laid, 0.0)
+    row_count[...] = jnp.full(row_count.shape, jnp.sum(mask), jnp.float32)
+    counts[me] = row_count[...]
+
+    acts = acts_ref[...]
+    gate = jnp.dot(acts, wg_ref[...], preferred_element_type=jnp.float32)
+    up = jnp.dot(acts, wu_ref[...], preferred_element_type=jnp.float32)
+    hidden_grad = lax.dot_general(
+        cot_ref[...], wd_ref[...], (((1,), (1,)), ((), ())), preferred_element_type=jnp.float32
+    )
+    sig = jax.nn.sigmoid(gate)
+    activated = gate * sig
+    hidden = activated * up
+    gate_grad = hidden_grad * up * sig * (1.0 + gate * (1.0 - sig))
+    up_grad = hidden_grad * activated
+    for block, values in enumerate((gate_grad, up_grad, hidden)):
+        turned = jnp.transpose(values)
+        for m in range(micro):
+            masked[block, m * width : (m + 1) * width, :] = (turned * mask[m : m + 1, :]).astype(jnp.bfloat16)
+
+    pl.semaphore_wait(barrier, everyone - 1)
+
+    def count_copy(step):
+        to = (me + step) % replicas
+        return pltpu.make_async_remote_copy(
+            src_ref=row_count, dst_ref=counts.at[me], send_sem=count_send.at[step],
+            recv_sem=count_recv.at[step], device_id=(section, to), device_id_type=MESH,
+        )
+
+    def send_count(step, carry):
+        count_copy(step).start()
+        return carry
+
+    lax.fori_loop(1, replicas, send_count, 0)
+
+    def pair_copy(k):
+        return pltpu.make_async_remote_copy(
+            src_ref=stage.at[k, pl.ds(pl.multiple_of((1 - core) * half, 8), half)], dst_ref=pair_in.at[k],
+            send_sem=pair_send.at[k], recv_sem=pair_recv.at[k], device_id=pair, device_id_type=MESH,
+        )
+
+    def x_copy(k, s):
+        return pltpu.make_async_remote_copy(
+            src_ref=x_out.at[k, pl.ds(s * piece, piece)], dst_ref=x_in.at[k, pl.ds(s * piece, piece)],
+            send_sem=x_send.at[k, s], recv_sem=x_recv.at[k, s], device_id=across, device_id_type=MESH,
+        )
+
+    def z_copy(k, s, way, to):
+        step = 1 - 2 * way
+        return pltpu.make_async_remote_copy(
+            src_ref=total.at[k, pl.ds(s * piece, piece)], dst_ref=z_in.at[way, to, pl.ds(s * piece, piece)],
+            send_sem=z_send.at[k, s], recv_sem=z_recv.at[way, to, s],
+            device_id=(section, me + 4 * step), device_id_type=MESH,
+        )
+
+    lane = lax.broadcasted_iota(jnp.int32, (rows // 2, LANES), 1)
+
+    def compute(k):
+        to = looked_up(order, z, k % line)
+        side = jnp.where(k < line, 1 - x, x)
+        start = pl.multiple_of((to * tiles + side * (whole + 1)) * LANES, LANES)
+        middle = pl.multiple_of((to * tiles + whole) * LANES, LANES)
+        shared = []
+        for block in range(3):
+            ref = cot_ref if block == 2 else acts_ref
+            taken = jnp.concatenate([ref[:, pl.ds(start, whole * LANES)], ref[:, pl.ds(middle, LANES)]], axis=1)
+            product = jnp.dot(masked[block], taken, preferred_element_type=jnp.float32)
+            rounded = product.astype(jnp.bfloat16).astype(jnp.float32)
+            summed = rounded[:width]
+            for m in range(1, micro):
+                summed = summed + rounded[m * width : (m + 1) * width]
+            for j in range(whole):
+                stage[k, j * rows + block * width : j * rows + (block + 1) * width, :] = summed[:, j * LANES : (j + 1) * LANES]
+            shared.append(summed[:, whole * LANES :])
+        shared = jnp.concatenate(shared, axis=0)
+        upper, lower = shared[: rows // 2], shared[rows // 2 :]
+        near = jnp.where(side == 0, upper, pltpu.roll(upper, LANES // 2, 1))
+        far = jnp.where(side == 0, pltpu.roll(lower, LANES // 2, 1), lower)
+        stage[k, whole * rows : whole * rows + rows // 2, :] = jnp.where(lane < LANES // 2, near, far)
+        pair_copy(k).start()
+
+    def merge(k):
+        pair_copy(k).wait_recv()
+        value = stage[k, pl.ds(pl.multiple_of(core * half, 8), half)] + pair_in[k]
+
+        @pl.when(k < line)
+        def _():
+            x_out[k] = value
+            for s in range(PIECES):
+                x_copy(k, s).start()
+
+        @pl.when(k >= line)
+        def _():
+            total[k - line] = value
+
+    def chunk(k, carry):
+        @pl.when(k < 2 * line)
+        def _():
+            compute(k)
+
+        @pl.when(k >= 1)
+        def _():
+            merge(k - 1)
+
+        return carry
+
+    lax.fori_loop(0, 2 * line + 1, chunk, 0)
+
+    def wait_count(step, carry):
+        count_copy(step).wait_recv()
+        return carry
+
+    def pass_on(k, carry):
+        to = looked_up(order, z, k)
+        up_way = to > z
+        way = jnp.where(up_way, 0, 1)
+        behind = jnp.where(up_way, z > 0, z < line - 1)
+        for s in range(PIECES):
+            at = pl.ds(s * piece, piece)
+            x_copy(k, s).wait_recv()
+            total[k, at] = total[k, at] + x_in[k, at]
+
+            @pl.when(behind)
+            def _():
+                z_copy(k, s, way, to).wait_recv()
+                total[k, at] = total[k, at] + z_in[way, to, at]
+
+            z_copy(k, s, way, to).start()
+        return carry
+
+    lax.fori_loop(0, line - 1, pass_on, 0)
+    lax.fori_loop(1, replicas, wait_count, 0)
+    count = counts[0]
+    for r in range(1, replicas):
+        count = count + counts[r]
+    inverse = count[0:1]
+
+    def full_copy(s):
+        at = pl.ds(pl.multiple_of(core * half + s * piece, 8), piece)
+        return pltpu.make_async_remote_copy(
+            src_ref=full.at[at], dst_ref=full.at[at], send_sem=full_send.at[s], recv_sem=full_recv.at[s],
+            device_id=pair, device_id_type=MESH,
+        )
+
+    last = line - 1
+    square = jnp.zeros((8, LANES), jnp.float32)
+    for s in range(PIECES):
+        at = pl.ds(s * piece, piece)
+        x_copy(last, s).wait_recv()
+        total[last, at] = total[last, at] + x_in[last, at]
+        for way in range(2):
+            @pl.when((z > 0) if way == 0 else (z < line - 1))
+            def _(way=way):
+                z_copy(last, s, way, z).wait_recv()
+                total[last, at] = total[last, at] + z_in[way, z, at]
+
+        scaled = total[last, at] / inverse
+        full[pl.ds(pl.multiple_of(core * half + s * piece, 8), piece)] = scaled
+        full_copy(s).start()
+        square = square + jnp.sum((scaled * scaled).reshape(piece // 8, 8, LANES), axis=0)
+    row_square[...] = square
+    squares[mine] = square
+
+    def square_copy(step):
+        to = (mine + step) % everyone
+        return pltpu.make_async_remote_copy(
+            src_ref=row_square, dst_ref=squares.at[mine], send_sem=square_send.at[step],
+            recv_sem=square_recv.at[step], device_id=(to // replicas, to % replicas), device_id_type=MESH,
+        )
+
+    def send_square(step, carry):
+        square_copy(step).start()
+        return carry
+
+    lax.fori_loop(1, everyone, send_square, 0)
+
+    for s in range(PIECES):
+        full_copy(s).wait_recv()
+    packed = full[whole * rows : whole * rows + rows // 2, :]
+    rolled = pltpu.roll(packed, LANES // 2, 1)
+    shared = jnp.concatenate([jnp.where(x == 0, packed, rolled), jnp.where(x == 0, rolled, packed)], axis=0)
+    main = [full[j * rows : (j + 1) * rows, :] for j in range(whole)]
+    span = tiles * LANES // 4
+    for side in range(2):
+        laid_out = main + [shared] if side == 0 else [shared] + main
+        for which in range(2):
+            @pl.when((x == side) & (core == which))
+            def _(laid_out=laid_out, side=side, which=which):
+                window = lane_window(laid_out, side * (LANES // 2) + which * span, out_ref.shape[1] // LANES)
+                for i, tile in enumerate(window):
+                    out_ref[:, i * LANES : (i + 1) * LANES] = tile
+
+    def wait_rest(k, carry):
+        pair_copy(k).wait_send()
+        return carry
+
+    lax.fori_loop(0, 2 * line, wait_rest, 0)
+    for s in range(PIECES):
+        full_copy(s).wait_send()
+        for k in range(line):
+            x_copy(k, s).wait_send()
+        for k in range(line - 1):
+            z_copy(k, s, jnp.where(z > 0, 1, 0), z).wait_send()
+
+    def wait_sent_count(step, carry):
+        count_copy(step).wait_send()
+        return carry
+
+    lax.fori_loop(1, replicas, wait_sent_count, 0)
+
+    def wait_squares(step, carry):
+        square_copy(step).wait()
+        return carry
+
+    lax.fori_loop(1, everyone, wait_squares, 0)
+    total_square = squares[0]
+    for r in range(1, everyone):
+        total_square = total_square + squares[r]
+    summed_square = jnp.sum(jnp.sum(total_square, axis=1, keepdims=True), axis=0, keepdims=True)
+    rms_ref[...] = jnp.broadcast_to(jnp.sqrt(summed_square / entries), rms_ref.shape)
+
+
+def fused(line, activations, cotangent, target_ids, w_gate, w_up, w_down):
+    _, micro, tokens, model = activations.shape
+    width = w_gate.shape[2]
+    sections, replicas = lax.axis_size("section"), lax.axis_size("dp")
+    rows = 3 * width
+    span = model // replicas
+    lanes = -(-span // LANES) * LANES
+    packed = rows * (model // line // 2) // LANES
+    half = packed // 2
+    entries = float(sections * rows * model)
+    vmem = pl.BlockSpec(memory_space=pltpu.VMEM)
+    f32, dma = jnp.float32, pltpu.SemaphoreType.DMA
+    out, rms = pl.pallas_call(
+        functools.partial(kernel, line, entries),
+        out_shape=(jax.ShapeDtypeStruct((rows, lanes), f32), jax.ShapeDtypeStruct((8, LANES), f32)),
+        in_specs=[vmem] * 6,
+        out_specs=(vmem, vmem),
+        scratch_shapes=[
+            pltpu.VMEM((3, micro * width, micro * tokens), jnp.bfloat16),
+            pltpu.VMEM((2 * line, packed, LANES), f32),
+            pltpu.VMEM((2 * line, half, LANES), f32),
+            pltpu.VMEM((line, half, LANES), f32),
+            pltpu.VMEM((line, half, LANES), f32),
+            pltpu.VMEM((line, half, LANES), f32),
+            pltpu.VMEM((2, line, half, LANES), f32),
+            pltpu.VMEM((packed, LANES), f32),
+            pltpu.VMEM((replicas, 8, LANES), f32),
+            pltpu.VMEM((sections * replicas, 8, LANES), f32),
+            pltpu.VMEM((8, LANES), f32),
+            pltpu.VMEM((8, LANES), f32),
+            dma((2 * line,)), dma((2 * line,)),
+            dma((line, PIECES)), dma((line, PIECES)),
+            dma((line, PIECES)), dma((2, line, PIECES)),
+            dma((PIECES,)), dma((PIECES,)),
+            dma((replicas,)), dma((replicas,)),
+            dma((sections * replicas,)), dma((sections * replicas,)),
+        ],
+        compiler_params=pltpu.CompilerParams(
+            collective_id=0, has_side_effects=True, vmem_limit_bytes=48 * 1024 * 1024
+        ),
+    )(
+        target_ids,
+        activations[0].reshape(micro * tokens, model),
+        cotangent[0].reshape(micro * tokens, model),
+        w_gate[0], w_up[0], w_down[0],
+    )
+    grad_gate = jnp.transpose(out[:width, :span])[None]
+    grad_up = jnp.transpose(out[width : 2 * width, :span])[None]
+    grad_down = out[2 * width :, :span][None]
+    return (grad_gate, grad_up, grad_down, rms[0, 0])
 
 
 def own_rows(product, span, axis):
@@ -75,6 +423,17 @@
     return (grad_gate, grad_up, grad_down, grad_rms)
 
 
+def line_length(mesh, model, width):
+    replicas = mesh.shape["dp"]
+    line = replicas // 4
+    if replicas % 4 or line < 2 or mesh.shape["section"] != 2:
+        return None
+    if model % (line * LANES) or (model // line // LANES) % 2 == 0:
+        return None
+    packed = 3 * width * (model // line // 2)
+    return line if packed % (2 * PIECES * 8 * LANES) == 0 else None
+
+
 def solution(mesh):
     in_specs = (
         P("section", None, "dp", None),
@@ -85,4 +444,10 @@
         P("section", None, None),
     )
     out_specs = (P("section", "dp", None), P("section", "dp", None), P("section", None, "dp"), P())
-    return jax.shard_map(shards, mesh=mesh, in_specs=in_specs, out_specs=out_specs, check_vma=False)
+
+    def program(*arrays):
+        line = line_length(mesh, arrays[3].shape[1], arrays[3].shape[2])
+        body = shards if line is None else functools.partial(fused, line)
+        return jax.shard_map(body, mesh=mesh, in_specs=in_specs, out_specs=out_specs, check_vma=False)(*arrays)
+
+    return program

time: 161 us -> 48.1 us (0.30)
  blocking collectives: 72.1 us -> 0 us
  waiting for transfers between devices: 47.6 us -> 0 us
  Pallas kernels: 0 us -> 41.6 us
  between operations: 15.9 us -> 0.71 us
  matrix products: 9.76 us -> 0 us
  other arithmetic: 7.33 us -> 0 us
  local copies, waits for them, and re-layouts: 7.61 us -> 5.66 us
    psum x3 -> x0, blocking collectives: 72.1 us -> none  [the longest x1 35.6 us: shards(): count = lax.psum(local_count, 'dp')]
    unnamed x2 -> x0, waiting for transfers between devices: 47.6 us -> none
    pallas_call x0 -> x1, Pallas kernels: none -> 41.6 us  [fused(): pl.pallas_call(functools.partial(kernel, line, entries), out_shape=(jax.S...]
    dot_general x6 -> x0, matrix products: 9.76 us -> none  [the longest x1 1.81 us: shards(): jnp.einsum('mtd,hd->mth', upstream, down_weight, preferred_element_type=j...]
    reduce_sum x4 -> x0, other arithmetic: 5.05 us -> none  [the longest x2 2.36 us: finalize_totals(): return jnp.sum(rounded.astype(jnp.float32), axis=0)]
    unnamed x6 -> x10, local copies, waits for them, and re-layouts: 6.9 us -> 4.44 us
    concatenate x1 -> x0, other arithmetic: 2.27 us -> none  [block_terms(): jnp.concatenate([part_gate, part_up, partial_lowering_weight], axis=1)]
  transfers between devices with their start and end apart: 1 -> 0, of which waited for: 1 -> 0; matrix products, arithmetic and copies ran while one was open for 0% -> 0% of each run, Pallas kernels for 0% -> 0%
where the time goes in v1:
time: 48.1 us; the launch traced here: 47.9 us
  Pallas kernels  41.6 us (86%)
  local copies, waits for them, and re-layouts  5.66 us (12%)
  between operations  0.71 us (1%)
    pallas_call x1, Pallas kernels, fused(): pl.pallas_call(functools.partial(kernel, line, entries), out_shape=(jax.S...  41.6 us
    unnamed x10, local copies, waits for them, and re-layouts  4.44 us

profile of v1, /device:TPU:0, one launch (start us, length us, event | category | flops | bytes accessed | tf_op | source)
XLA Modules:
  0.0 47.9 jit_solution(6271815665569288607)
XLA Ops:
  0.6 0.0 copy-start.3
  0.6 1.5 %copy.10 = bf16[1,3584,96]{2,1,0:T(8,128)(2,1)S(1)} copy(bf16[1,3584,96]{1,2,0:T(8,128)(2,1)} %param.9) | data formatting | bytes 1376256 | tf_op args[3]
  2.2 0.0 copy-start
  2.2 0.0 copy-start.2
  2.2 1.7 %copy.11 = bf16[1,3584,96]{2,1,0:T(8,128)(2,1)S(1)} copy(bf16[1,3584,96]{1,2,0:T(8,128)(2,1)} %param.10) | data formatting | bytes 1376256 | tf_op args[4]
  3.9 0.0 copy-done.3
  3.9 0.0 copy-done
  3.9 0.0 copy-done.2
  4.0 0.0 copy-start.1
  4.0 1.2 %copy-done.1 = bf16[1,8,16,3584]{3,2,1,0:T(8,128)(2,1)S(1)} copy-done((bf16[1,8,16,3584]{3,2,1,0:T(8,128)(2,1)S(1)}, bf16[1,8,16,3584]{3,2,1,0:T(8,128)(2,1)}, u32[]{:S(2)}) %copy-start.1) | copy-done | bytes 917528
  5.1 41.6 %shard_map.93 = (f32[288,256]{1,0:T(8,128)S(1)}, f32[8,128]{1,0:T(8,128)S(1)}) custom-call(s32[8,16]{1,0:T(8,128)S(1)} %copy-done.3, bf16[128,3584]{1,0:T(8,128)(2,1)S(1)} %bitcast.18, bf16[128,3584]{1,0:T(8,128)(2,1)S(1)} %bitcast.19, bf16[3584,96]{1,0:T(8,128)(2,1)S(1)} %bitcast.16, bf16[3584,96]{1,0:T(8,128)(2,1)S(1)} %bitcast.17, ...), custom_call_target="tpu_custom_call" | custom-call | tf_op jit(solution)/shard_map/pallas_call | solution.py:315
  46.7 0.5 %slice.15 = f32[1,1]{1,0:T(1,128)} slice(f32[8,128]{1,0:T(8,128)S(1)} %get-tuple-element.7), slice={[0:1], [0:1]} | slice | bytes 8 | tf_op jit(solution)/shard_map/slice | solution.py:352
  47.2 0.7 %slice_bitcast_fusion = (f32[1,96,224]{2,1,0:T(8,128)}, f32[1,224,96]{1,2,0:T(8,128)}, f32[1,224,96]{1,2,0:T(8,128)}) fusion(f32[288,256]{1,0:T(8,128)S(1)} %get-tuple-element.6), kind=kLoop, calls=%fused_computation | loop fusion | bytes 516096 | tf_op jit(solution)/shard_map/broadcast_in_dim | solution.py:351
Async XLA Ops:
  0.6 3.3 %copy-start.3 = (s32[8,16]{1,0:T(8,128)S(1)}, s32[8,16]{1,0:T(8,128)}, u32[]{:S(2)}) copy-start(s32[8,16]{1,0:T(8,128)} %ids_ref.1) | copy-start | bytes 1540
  2.2 1.7 %copy-start = (bf16[1,8,16,3584]{3,2,1,0:T(8,128)(2,1)S(1)}, bf16[1,8,16,3584]{3,2,1,0:T(8,128)(2,1)}, u32[]{:S(2)}) copy-start(bf16[1,8,16,3584]{3,2,1,0:T(8,128)(2,1)} %param.6) | copy-start | bytes 2752516
  2.2 1.7 %copy-start.2 = (bf16[1,96,3584]{2,1,0:T(8,128)(2,1)S(1)}, bf16[1,96,3584]{2,1,0:T(8,128)(2,1)}, u32[]{:S(2)}) copy-start(bf16[1,96,3584]{2,1,0:T(8,128)(2,1)} %param.11) | copy-start | bytes 2064388
  4.0 1.2 %copy-start.1 = (bf16[1,8,16,3584]{3,2,1,0:T(8,128)(2,1)S(1)}, bf16[1,8,16,3584]{3,2,1,0:T(8,128)(2,1)}, u32[]{:S(2)}) copy-start(bf16[1,8,16,3584]{3,2,1,0:T(8,128)(2,1)} %param.7) | copy-start | bytes 2752516
